TPU v7x, 128 devices: a whole 4x4x4 slice. The times are simulated.
128 devices in a mesh: grp: 32 (over y, z_hi, x), sub: 4 (over z_lo, core).
Axes of the slice: x: 4, y: 4, z: 4 (z_hi: 2, z_lo: 2; z = z_hi * 2 + z_lo), core: 2. Of those that a mesh axis runs over, the one named last changes fastest.
Arguments:
- master: float32 [16384, 3584], P(('grp', 'sub')), may hold values from -120 to 120
- moment_one: float32 [16384, 3584], P(('grp', 'sub')), may hold values from -6 to 6
- moment_two: float32 [16384, 3584], P(('grp', 'sub')), may hold values from 0.01 to 4
- gradient: float32 [16384, 3584], P(('grp', 'sub')), may hold values from -120 to 120
- partner: int32 [128], replicated, may hold values from 0 to 127, each once
- tensor_of_row: int32 [16384], replicated, may hold values from 0 to 7, never falling along the last dimension, each value on 1 to 4096 neighbouring positions
Outputs:
- new_master: float32 [16384, 3584], P(('grp', 'sub'))
- new_moment_one: float32 [16384, 3584], P(('grp', 'sub'))
- new_moment_two: float32 [16384, 3584], P(('grp', 'sub'))
Inputs may be any that keep to these rules, and one draw needn't show every extreme that they name: partner[n] is the device of new rank n; every device holds exactly one rank. `tensor_of_row`: tensor numbers never fall along the rows; each of the 8 tensors has one or more rows.
All inputs are finite; a program needn't handle non-finite values.
Results may differ from a plain program's by a relative error of at most 0.00007.
Values sent between devices are 32-bit elements; how exact they have to be, the bound alone decides.
A program may use at most 128 MiB of HBM per device.

v0:
```python
import functools

import jax
import jax.numpy as jnp
from jax import lax
from jax.sharding import Mesh
from jax.sharding import PartitionSpec as P

LAYERS = 8
GRP_SUB = ("grp_0", "grp_1", "grp_2", "sub_0", "sub_1")


beta_one = 0.9
beta_two = 0.999
step_count = 10
adam_eps = 1e-06
trust_eps = 1e-06
learn_rate = 0.05
decay_rate = 0.01


def one_axis_at_a_time(x, axes):
    return functools.reduce(lax.psum, axes, x)


def tensor_totals(values, onehot):
    return jnp.dot(values[None, :], onehot, precision=lax.Precision.HIGHEST)[0]


def local(master, moment_one, moment_two, gradient, partner, tensor_of_row):
    rows_dev, width = master.shape
    devices = lax.axis_size(GRP_SUB)
    block = rows_dev // devices
    device_id = lax.axis_index(GRP_SUB)
    numbers = jnp.arange(devices, dtype=jnp.int32)
    matches = partner[None, :] == numbers[:, None]
    inverse = jnp.sum(jnp.where(matches, numbers[None, :], 0), axis=1)
    my_rank = lax.dynamic_index_in_dim(inverse, device_id, 0, keepdims=False)
    layer_ids = jnp.arange(LAYERS, dtype=jnp.int32)
    id_grid = tensor_of_row.reshape(devices, devices, block)
    new_ids = lax.dynamic_index_in_dim(id_grid, my_rank, 1, keepdims=False).reshape(rows_dev)
    new_hot = (new_ids[:, None] == layer_ids[None, :]).astype(jnp.float32)

    def outbound(values):
        return jnp.take(values.reshape(devices, block, width), inverse, axis=0)

    sending = (outbound(master), outbound(moment_one), outbound(moment_two))
    arrived = (
        lax.all_to_all(sending[0], GRP_SUB, split_axis=0, concat_axis=0, tiled=True),
        lax.all_to_all(sending[1], GRP_SUB, split_axis=0, concat_axis=0, tiled=True),
        lax.all_to_all(sending[2], GRP_SUB, split_axis=0, concat_axis=0, tiled=True),
    )
    weights, moment_old, square_old = [piece.reshape(rows_dev, width) for piece in arrived]
    first = beta_one * moment_old + (1.0 - beta_one) * gradient
    second = beta_two * square_old + (1.0 - beta_two) * gradient * gradient
    correct_one = 1.0 - beta_one**step_count
    correct_two = 1.0 - beta_two**step_count
    update = (
        first / correct_one / (jnp.sqrt(second / correct_two) + adam_eps) + decay_rate * weights
    )
    update_local = tensor_totals(jnp.sum(update * update, axis=1), new_hot)
    weight_local = tensor_totals(jnp.sum(weights * weights, axis=1), new_hot)
    weight_sq, update_sq = (
        one_axis_at_a_time(weight_local, GRP_SUB),
        one_axis_at_a_time(update_local, GRP_SUB),
    )
    ratio = jnp.sqrt(weight_sq) / (jnp.sqrt(update_sq) + trust_eps)
    row_ratio = jnp.dot(new_hot, ratio[:, None], precision=lax.Precision.HIGHEST)
    fresh = weights - learn_rate * row_ratio * update
    return (fresh, first, second)


def solution(mesh):
    finer = Mesh(mesh.devices.reshape(4, 2, 4, 2, 2), ("grp_0", "grp_1", "grp_2", "sub_0", "sub_1"))
    in_specs = (P(GRP_SUB, None), P(GRP_SUB, None), P(GRP_SUB, None), P(GRP_SUB, None), P(), P())
    out_specs = (P(GRP_SUB, None), P(GRP_SUB, None), P(GRP_SUB, None))
    return jax.shard_map(local, mesh=finer, in_specs=in_specs, out_specs=out_specs, check_vma=False)
```

profile of v0, /device:TPU:1, one launch (start us, length us, event | category | flops | bytes accessed | tf_op | source)
XLA Modules:
  0.0 169.4 jit_solution(15982042428079250486)
XLA Ops:
  0.6 0.0 copy-start
  0.6 0.9 select_reduce_fusion
  1.6 0.6 copy-done
  2.2 2.4 %gather_fusion.2 = f32[128,3584]{1,0:T(8,128)} fusion(f32[128,3584]{1,0:T(8,128)S(1)} %copy-done, s32[1024]{0:T(1024)S(1)} %pad_clamp_fusion), kind=kCustom, calls=%fused_computation.2.clone | custom fusion | bytes 3670528 | tf_op jit(solution)/shard_map/jit(_take)/gather | solution.py:45
  4.6 4.7 %gather_fusion.1 = f32[128,3584]{1,0:T(8,128)} fusion(f32[128,3584]{1,0:T(8,128)} %param.9, s32[1024]{0:T(1024)S(1)} %pad_clamp_fusion), kind=kCustom, calls=%fused_computation.1.clone | custom fusion | bytes 3670528 | tf_op jit(solution)/shard_map/jit(_take)/gather | solution.py:45
  9.2 4.7 %gather_fusion = f32[128,3584]{1,0:T(8,128)} fusion(f32[128,3584]{1,0:T(8,128)} %param.8, s32[1024]{0:T(1024)S(1)} %pad_clamp_fusion), kind=kCustom, calls=%fused_computation.clone | custom fusion | bytes 3670528 | tf_op jit(solution)/shard_map/jit(_take)/gather | solution.py:45
  13.9 5.0 %bitcast_select_fusion = (f32[128,1,3584]{2,0,1:T(8,128)S(1)}, f32[128,1,3584]{2,0,1:T(8,128)}, f32[128,1,3584]{2,0,1:T(8,128)}) fusion(f32[128,3584]{1,0:T(8,128)} %gather_fusion.2, pred[128]{0:T(512)(128)(4,1)S(1)} %compare_and_fusion, f32[128,3584]{1,0:T(8,128)} %gather_fusion.1, f32[128,3584]{1,0:T(8,128)} %gather_fusion), kind=kLoop, calls=%fused_computation.10 | loop fusion | flops 1376256 | bytes 11010176 | tf_op jit(solution)/shard_map/jit(_take)/select_n | solution.py:45
  18.9 3.1 %copy.17 = f32[128,1,3584]{2,1,0:T(1,128)} copy(f32[128,1,3584]{2,0,1:T(8,128)S(1)} %get-tuple-element.19) | data formatting | bytes 3670016 | tf_op jit(solution)/shard_map/jit(_take)/select_n | solution.py:45
  22.0 11.9 %all-to-all-start.2 = ((f32[128,1,3584]{2,1,0:T(1,128)}), f32[128,1,3584]{2,1,0:T(1,128)}, u32[]{:S(2)}, u32[]{:S(2)}) async-start(f32[128,1,3584]{2,1,0:T(1,128)} %copy.17), calls=%async_computation.2 | async-start | bytes 3670016 | tf_op jit(solution)/shard_map/all_to_all | solution.py:51
  33.9 4.6 %copy.15 = f32[128,1,3584]{2,1,0:T(1,128)} copy(f32[128,1,3584]{2,0,1:T(8,128)} %get-tuple-element.20) | data formatting | bytes 3670016 | tf_op jit(solution)/shard_map/jit(_take)/select_n | solution.py:45
  38.5 22.3 %all-to-all-done.2 = f32[128,1,3584]{2,1,0:T(1,128)} async-done(((f32[128,1,3584]{2,1,0:T(1,128)}), f32[128,1,3584]{2,1,0:T(1,128)}, u32[]{:S(2)}, u32[]{:S(2)}) %all-to-all-start.2) | async-done | bytes 1835040 | tf_op jit(solution)/shard_map/all_to_all | solution.py:51
  60.8 5.4 %all-to-all-start.1 = ((f32[128,1,3584]{2,1,0:T(1,128)}), f32[128,1,3584]{2,1,0:T(1,128)}, u32[]{:S(2)}, u32[]{:S(2)}) async-start(f32[128,1,3584]{2,1,0:T(1,128)} %copy.15), calls=%async_computation.1 | async-start | bytes 3670016 | tf_op jit(solution)/shard_map/all_to_all | solution.py:50
  66.3 4.6 %copy.14 = f32[128,1,3584]{2,1,0:T(1,128)} copy(f32[128,1,3584]{2,0,1:T(8,128)} %get-tuple-element.21) | data formatting | bytes 3670016 | tf_op jit(solution)/shard_map/jit(_take)/select_n | solution.py:45
  70.9 0.0 copy-start.1
  70.9 22.4 %all-to-all-done.1 = f32[128,1,3584]{2,1,0:T(1,128)} async-done(((f32[128,1,3584]{2,1,0:T(1,128)}), f32[128,1,3584]{2,1,0:T(1,128)}, u32[]{:S(2)}, u32[]{:S(2)}) %all-to-all-start.1) | async-done | bytes 1835040 | tf_op jit(solution)/shard_map/all_to_all | solution.py:50
  93.3 5.6 %all-to-all-start = ((f32[128,1,3584]{2,1,0:T(1,128)}), f32[128,1,3584]{2,1,0:T(1,128)}, u32[]{:S(2)}, u32[]{:S(2)}) async-start(f32[128,1,3584]{2,1,0:T(1,128)} %copy.14), calls=%async_computation | async-start | bytes 3670016 | tf_op jit(solution)/shard_map/all_to_all | solution.py:49
  99.0 0.6 dynamic_slice.8
  101.5 0.0 copy-done.1
  101.5 0.2 dynamic-slice_reduce_fusion
  101.7 24.3 %all-to-all-done = f32[128,1,3584]{2,1,0:T(1,128)} async-done(((f32[128,1,3584]{2,1,0:T(1,128)}), f32[128,1,3584]{2,1,0:T(1,128)}, u32[]{:S(2)}, u32[]{:S(2)}) %all-to-all-start) | async-done | bytes 1835040 | tf_op jit(solution)/shard_map/all_to_all | solution.py:49
  126.0 7.1 %multiply_reduce_fusion = (f32[128]{0:T(128)S(1)}, f32[128,3584]{1,0:T(8,128)}, f32[128,3584]{1,0:T(8,128)}, f32[128,3584]{1,0:T(8,128)}, f32[128]{0:T(128)S(1)}) fusion(f32[128,1,3584]{2,1,0:T(1,128)} %all-to-all-done, f32[128,3584]{1,0:T(8,128)} %param.11, f32[128,1,3584]{2,1,0:T(1,128)} %all-to-all-done.1, f32[128,1,3584]{2,1,0:T(1,128)} %all-to-all-done.2), kind=kLoop, calls=%fused_computation.16 | loop fusion | flops 7798528 | bytes 12846080 | tf_op jit(solution)/shard_map/reduce_sum | solution.py:61
  133.1 0.2 convolution_bitcast_fusion.1
  133.3 0.2 convolution_bitcast_fusion.2
  133.5 6.9 %all-reduce.1 = (f32[8]{0:T(128)S(1)}, f32[8]{0:T(128)S(1)}) all-reduce(f32[8]{0:T(128)S(1)} %convolution_bitcast_fusion.1, f32[8]{0:T(128)S(1)} %convolution_bitcast_fusion.2), channel_id=1, replica_groups=mesh['grp_0'=4,'grp_1'=2,'grp_2'=4,'sub_0'=2,'sub_1'=2] {'grp_0'}, use_global_device_ids=true, to_apply=%region_8.10 | all-reduce | flops 16 | bytes 128 | tf_op jit(solution)/shard_map/psum | solution.py:23
  140.4 5.3 %all-reduce.4 = (f32[8]{0:T(128)S(1)}, f32[8]{0:T(128)S(1)}) all-reduce(f32[8]{0:T(128)S(1)} %get-tuple-element.6, f32[8]{0:T(128)S(1)} %get-tuple-element.7), channel_id=1, replica_groups=mesh['grp_0'=4,'grp_1'=2,'grp_2'=4,'sub_0'=2,'sub_1'=2] {'grp_1'}, use_global_device_ids=true, to_apply=%region_9.11 | all-reduce | flops 16 | bytes 128 | tf_op jit(solution)/shard_map/psum | solution.py:23
  145.7 6.6 %all-reduce = (f32[8]{0:T(128)S(1)}, f32[8]{0:T(128)S(1)}) all-reduce(f32[8]{0:T(128)S(1)} %get-tuple-element.12, f32[8]{0:T(128)S(1)} %get-tuple-element.13), channel_id=1, replica_groups=mesh['grp_0'=4,'grp_1'=2,'grp_2'=4,'sub_0'=2,'sub_1'=2] {'grp_2'}, use_global_device_ids=true, to_apply=%region_10.12 | all-reduce | flops 16 | bytes 128 | tf_op jit(solution)/shard_map/psum | solution.py:23
  152.3 3.8 %all-reduce.3 = (f32[8]{0:T(128)S(1)}, f32[8]{0:T(128)S(1)}) all-reduce(f32[8]{0:T(128)S(1)} %get-tuple-element.4, f32[8]{0:T(128)S(1)} %get-tuple-element.5), channel_id=1, replica_groups=mesh['grp_0'=4,'grp_1'=2,'grp_2'=4,'sub_0'=2,'sub_1'=2] {'sub_0'}, use_global_device_ids=true, to_apply=%region_11.13 | all-reduce | flops 16 | bytes 128 | tf_op jit(solution)/shard_map/psum | solution.py:23
  156.1 9.5 %all-reduce.2 = (f32[8]{0:T(128)S(1)}, f32[8]{0:T(128)S(1)}) all-reduce(f32[8]{0:T(128)S(1)} %get-tuple-element.10, f32[8]{0:T(128)S(1)} %get-tuple-element.11), channel_id=1, replica_groups=mesh['grp_0'=4,'grp_1'=2,'grp_2'=4,'sub_0'=2,'sub_1'=2] {'sub_1'}, use_global_device_ids=true, to_apply=%region_12.14 | all-reduce | flops 16 | bytes 128 | tf_op jit(solution)/shard_map/psum | solution.py:23
  165.6 0.2 fusion.3
  165.8 3.6 %bitcast_subtract_fusion = f32[128,3584]{1,0:T(8,128)} fusion(f32[128,3584]{1,0:T(8,128)} %get-tuple-element.15, f32[128,1,3584]{2,1,0:T(1,128)} %all-to-all-done, f32[128]{0:T(128)S(1)} %fusion.3), kind=kLoop, calls=%fused_computation.5 | loop fusion | flops 917504 | bytes 5505536 | tf_op jit(solution)/shard_map/sub | solution.py:69
  (3 shorter events, 0.0 us)
Async XLA Ops:
  0.6 1.5 copy-start
  22.0 38.8 %all-to-all-start.2 = ((f32[128,1,3584]{2,1,0:T(1,128)}), f32[128,1,3584]{2,1,0:T(1,128)}, u32[]{:S(2)}, u32[]{:S(2)}) async-start(f32[128,1,3584]{2,1,0:T(1,128)} %copy.17), calls=%async_computation.2 | async-start | bytes 3670016 | tf_op jit(solution)/shard_map/all_to_all | solution.py:51
  60.8 32.5 %all-to-all-start.1 = ((f32[128,1,3584]{2,1,0:T(1,128)}), f32[128,1,3584]{2,1,0:T(1,128)}, u32[]{:S(2)}, u32[]{:S(2)}) async-start(f32[128,1,3584]{2,1,0:T(1,128)} %copy.15), calls=%async_computation.1 | async-start | bytes 3670016 | tf_op jit(solution)/shard_map/all_to_all | solution.py:50
  70.9 30.6 %copy-start.1 = (s32[16384]{0:T(1024)S(1)}, s32[16384]{0:T(1024)}, u32[]{:S(2)}) copy-start(s32[16384]{0:T(1024)} %param.13) | copy-start | bytes 196612
  93.3 32.7 %all-to-all-start = ((f32[128,1,3584]{2,1,0:T(1,128)}), f32[128,1,3584]{2,1,0:T(1,128)}, u32[]{:S(2)}, u32[]{:S(2)}) async-start(f32[128,1,3584]{2,1,0:T(1,128)} %copy.14), calls=%async_computation | async-start | bytes 3670016 | tf_op jit(solution)/shard_map/all_to_all | solution.py:49
where the time goes:
time: 170 us; the launch traced here: 169 us
  waiting for transfers between devices  69.1 us (41%)
  blocking collectives  32.1 us (19%)
  local copies, waits for them, and re-layouts  25.4 us (15%)
  starting transfers between devices  22.9 us (13%)
  other arithmetic  16.6 us (10%)
  between operations  2.67 us (2%)
    psum x5, blocking collectives, one_axis_at_a_time(): return functools.reduce(lax.psum, axes, x)  32.1 us
    all_to_all x1, waiting for transfers between devices, local(): lax.all_to_all(sending[0], GRP_SUB, split_axis=0, concat_axis=0, tiled=True)  24.3 us
    all_to_all x1, waiting for transfers between devices, local(): lax.all_to_all(sending[1], GRP_SUB, split_axis=0, concat_axis=0, tiled=True)  22.4 us
    all_to_all x1, waiting for transfers between devices, local(): lax.all_to_all(sending[2], GRP_SUB, split_axis=0, concat_axis=0, tiled=True)  22.3 us
    select_n x3, local copies, waits for them, and re-layouts, outbound(): return jnp.take(values.reshape(devices, block, width), inverse, axis=0)  12.3 us
    all_to_all x1, starting transfers between devices, local(): lax.all_to_all(sending[2], GRP_SUB, split_axis=0, concat_axis=0, tiled=True)  11.9 us
    gather x3, local copies, waits for them, and re-layouts, outbound(): return jnp.take(values.reshape(devices, block, width), inverse, axis=0)  11.8 us
    reduce_sum x1, other arithmetic, local(): update_local = tensor_totals(jnp.sum(update * update, axis=1), new_hot)  7.06 us
  transfers between devices with their start and end apart: 3, of which 3 were waited for; matrix products, arithmetic and copies ran while one was open for 6% of the time, Pallas kernels for 0%

commit v1 on v0

v1 whole, which is shorter than its diff:
```python
import functools

import jax
import jax.numpy as jnp
from jax import lax
from jax.experimental import pallas as pl
from jax.experimental.pallas import tpu as pltpu
from jax.sharding import Mesh
from jax.sharding import PartitionSpec as P

LAYERS = 8
AXES = ("grp_0", "grp_1", "grp_2", "sub_0", "sub_1")
LOGICAL = pl.DeviceIdType.LOGICAL
STRIDE = 37
LANES = 128
GROUP = 8


beta_one = 0.9
beta_two = 0.999
step_count = 10
adam_eps = 1e-06
trust_eps = 1e-06
learn_rate = 0.05
decay_rate = 0.01


def own_place():
    y = lax.axis_index("grp_0")
    z = lax.axis_index("grp_1") * 2 + lax.axis_index("sub_0")
    x = lax.axis_index("grp_2")
    core = lax.axis_index("sub_1")
    return x, y, z, core


def number_of(x, y, z, core):
    return (((y * 2 + z // 2) * 4 + x) * 2 + z % 2) * 2 + core


def exchange_kernel(
    inverse, partner, row_tensor, master, moment_one, moment_two, gradient,
    weights, update, first, second, row_ratio,
    source, sending, spare, ids, partial, totals,
    load_sem, grad_sem, send_sem, recv_sem, total_send_sem, total_recv_sem,
):
    devices, width = weights.shape
    blocks = devices // GROUP
    x, y, z, core = own_place()
    me = number_of(x, y, z, core)
    arrived = (weights, first, second)

    def target(step):
        offset = (step * STRIDE) % devices
        return number_of(
            (x + offset // 32) % 4, (y + offset // 8 % 4) % 4, (z + offset // 2 % 4) % 4, (core + offset % 2) % 2
        )

    loads = [
        pltpu.make_async_copy(array, source.at[k], load_sem.at[k])
        for k, array in enumerate((master, moment_one, moment_two))
    ]
    for load in loads:
        load.start()
    grad_load = pltpu.make_async_copy(gradient, update, grad_sem)
    grad_load.start()

    barrier = pltpu.get_barrier_semaphore()

    def greet(step, carry):
        pl.semaphore_signal(barrier, inc=1, device_id=(me + step) % devices, device_id_type=LOGICAL)
        return carry

    lax.fori_loop(1, devices, greet, 0)

    held = lax.broadcasted_iota(jnp.int32, (devices, devices), 1)
    mine = jnp.where(partner[...] == me, row_tensor[...] + held * 0, 0)
    ids[...] = jnp.broadcast_to(jnp.sum(mine, axis=1, keepdims=True), (devices, LANES))

    for load in loads:
        load.wait()

    def pick(step):
        row = inverse[target(step)]
        for k in range(3):
            sending[k, pl.ds(step, 1), :] = source[k, pl.ds(row, 1), :]

    def send(step):
        there = target(step)
        for k in range(3):
            pltpu.make_async_remote_copy(
                src_ref=sending.at[k, pl.ds(step, 1)],
                dst_ref=arrived[k].at[pl.ds(me, 1)],
                send_sem=send_sem,
                recv_sem=recv_sem.at[me // GROUP],
                device_id=there,
                device_id_type=LOGICAL,
            ).start()

    for step in range(GROUP):
        pick(step)
    pl.semaphore_wait(barrier, devices - 1)

    def keep():
        for k in range(3):
            pltpu.make_async_copy(
                sending.at[k, pl.ds(0, 1)], arrived[k].at[pl.ds(me, 1)], recv_sem.at[me // GROUP]
            ).start()
            pltpu.make_async_copy(sending.at[k, pl.ds(0, 1)], spare.at[k, pl.ds(0, 1)], send_sem).start()

    def pick_group(group):
        for j in range(GROUP):
            pick(group * GROUP + j)

    pick_group(1)
    keep()
    for step in range(1, GROUP):
        send(step)

    def round_of(group, carry):
        pick_group(group + 1)
        for j in range(GROUP):
            send(group * GROUP + j)
        return carry

    lax.fori_loop(1, blocks - 1, round_of, 0)
    for j in range(GROUP):
        send((blocks - 1) * GROUP + j)

    grad_load.wait()
    scale_one = 1.0 / (1.0 - beta_one**step_count)
    scale_two = 1.0 / (1.0 - beta_two**step_count)

    def compute(block, sums):
        pltpu.make_async_copy(
            sending.at[0, pl.ds(0, 3 * GROUP)], source.at[0, pl.ds(0, 3 * GROUP)], recv_sem.at[block]
        ).wait()
        rows = pl.ds(pl.multiple_of(block * GROUP, GROUP), GROUP)
        row_update = jnp.zeros((GROUP, LANES), jnp.float32)
        row_weight = jnp.zeros((GROUP, LANES), jnp.float32)
        for lane in range(0, width, LANES):
            cols = pl.ds(lane, LANES)
            grad = update[rows, cols]
            weight = weights[rows, cols]
            new_first = beta_one * first[rows, cols] + (1.0 - beta_one) * grad
            new_second = beta_two * second[rows, cols] + (1.0 - beta_two) * grad * grad
            step = (new_first * scale_one) / (jnp.sqrt(new_second * scale_two) + adam_eps) + decay_rate * weight
            first[rows, cols] = new_first
            second[rows, cols] = new_second
            update[rows, cols] = step
            row_update += step * step
            row_weight += weight * weight
        tensor = ids[rows, :]
        return tuple(
            (
                sums[t][0] + jnp.where(tensor == t, row_update, 0.0),
                sums[t][1] + jnp.where(tensor == t, row_weight, 0.0),
            )
            for t in range(LAYERS)
        )

    zero = jnp.zeros((GROUP, LANES), jnp.float32)
    sums = lax.fori_loop(0, blocks, compute, tuple((zero, zero) for _ in range(LAYERS)))

    lane_id = lax.broadcasted_iota(jnp.int32, (1, LANES), 1)
    packed = jnp.zeros((1, LANES), jnp.float32)
    for t in range(LAYERS):
        for part in range(2):
            packed = jnp.where(lane_id == t + LAYERS * part, jnp.sum(sums[t][part]), packed)
    partial[...] = jnp.broadcast_to(packed, (GROUP, LANES))

    def tell(step, carry):
        pltpu.make_async_remote_copy(
            src_ref=partial.at[pl.ds(0, 1)],
            dst_ref=totals.at[pl.ds(me, 1)],
            send_sem=total_send_sem,
            recv_sem=total_recv_sem,
            device_id=target(step),
            device_id_type=LOGICAL,
        ).start()
        return carry

    lax.fori_loop(1, devices, tell, 0)
    pltpu.make_async_copy(partial.at[pl.ds(0, 1)], totals.at[pl.ds(me, 1)], total_recv_sem).start()
    pltpu.make_async_copy(partial.at[pl.ds(0, 1)], spare.at[0, pl.ds(1, 1), pl.ds(0, LANES)], total_send_sem).start()
    pltpu.make_async_copy(totals, totals, total_recv_sem).wait()
    summed = jnp.sum(totals[...], axis=0, keepdims=True)
    ratio = jnp.sqrt(pltpu.roll(summed, LANES - LAYERS, 1)) / (jnp.sqrt(summed) + trust_eps)
    hot = lax.broadcasted_iota(jnp.int32, (devices, LANES), 1) == ids[...]
    per_row = jnp.sum(jnp.where(hot, ratio, 0.0), axis=1, keepdims=True)
    row_ratio[...] = jnp.broadcast_to(per_row, (devices, LANES))

    pltpu.make_async_copy(sending, source, send_sem).wait()
    pltpu.make_async_copy(totals, totals, total_send_sem).wait()


def finish_kernel(weights, update, first, second, row_ratio, new_master, new_one, new_two, fresh, sem_one, sem_two, sem_fresh):
    rows, width = weights.shape
    one = pltpu.make_async_copy(first, new_one, sem_one)
    two = pltpu.make_async_copy(second, new_two, sem_two)
    one.start()
    two.start()
    chunk = 32
    writes = []
    for index in range(rows // chunk):
        at = pl.ds(index * chunk, chunk)
        scale = learn_rate * row_ratio[at, :]
        for lane in range(0, width, LANES):
            cols = pl.ds(lane, LANES)
            fresh[at, cols] = weights[at, cols] - scale * update[at, cols]
        writes.append(pltpu.make_async_copy(fresh.at[at], new_master.at[at], sem_fresh.at[index]))
        writes[-1].start()
    for write in writes:
        write.wait()
    one.wait()
    two.wait()


def local(master, moment_one, moment_two, gradient, partner, tensor_of_row):
    rows_dev, width = master.shape
    devices = partner.shape[0]
    numbers = jnp.arange(devices, dtype=jnp.int32)
    inverse = jnp.sum(jnp.where(partner[None, :] == numbers[:, None], numbers[None, :], 0), axis=1)
    vmem = pl.BlockSpec(memory_space=pltpu.VMEM)
    hbm = pl.BlockSpec(memory_space=pltpu.HBM)
    smem = pl.BlockSpec(memory_space=pltpu.SMEM)
    block = pltpu.VMEM((rows_dev, width), jnp.float32)
    stack = pltpu.VMEM((3, rows_dev, width), jnp.float32)
    dma = pltpu.SemaphoreType.DMA
    weights, update, first, second, row_ratio = pl.pallas_call(
        exchange_kernel,
        out_shape=(block, block, block, block, pltpu.VMEM((rows_dev, LANES), jnp.float32)),
        in_specs=[smem, vmem, vmem, hbm, hbm, hbm, hbm],
        out_specs=(vmem,) * 5,
        scratch_shapes=[
            stack,
            stack,
            pltpu.VMEM((3, GROUP, width), jnp.float32),
            pltpu.VMEM((rows_dev, LANES), jnp.int32),
            pltpu.VMEM((GROUP, LANES), jnp.float32),
            pltpu.VMEM((devices, LANES), jnp.float32),
            dma((3,)),
            dma,
            dma,
            dma((devices // GROUP,)),
            dma,
            dma,
        ],
        compiler_params=pltpu.CompilerParams(
            collective_id=0, has_side_effects=True, vmem_limit_bytes=24 * 1024 * 1024
        ),
        name="exchange",
    )(inverse, partner.reshape(1, devices), tensor_of_row.reshape(devices, devices), master, moment_one, moment_two, gradient)
    whole = jax.ShapeDtypeStruct((rows_dev, width), jnp.float32)
    return pl.pallas_call(
        finish_kernel,
        out_shape=(whole,) * 3,
        in_specs=[vmem] * 5,
        out_specs=(hbm,) * 3,
        scratch_shapes=[block, dma, dma, dma((4,))],
        compiler_params=pltpu.CompilerParams(vmem_limit_bytes=8 * 1024 * 1024),
        name="finish",
    )(weights, update, first, second, row_ratio)


def solution(mesh):
    finer = Mesh(mesh.devices.reshape(4, 2, 4, 2, 2), AXES)
    in_specs = (P(AXES, None), P(AXES, None), P(AXES, None), P(AXES, None), P(), P())
    out_specs = (P(AXES, None), P(AXES, None), P(AXES, None))
    return jax.shard_map(local, mesh=finer, in_specs=in_specs, out_specs=out_specs, check_vma=False)
```

time: 170 us -> 101 us (0.59)
  Pallas kernels: 0 us -> 91.3 us
  waiting for transfers between devices: 69.1 us -> 0 us
  blocking collectives: 32.1 us -> 0 us
  starting transfers between devices: 22.9 us -> 0 us
  local copies, waits for them, and re-layouts: 25.4 us -> 7.49 us
  other arithmetic: 16.6 us -> 0.76 us
  between operations: 2.67 us -> 0.66 us
    pallas_call x0 -> x2, Pallas kernels: none -> 91.3 us  [the longest x1 88.8 us: local(): pl.pallas_call(exchange_kernel, out_shape=(block, block, block, block, pl...]
    all_to_all x3 -> x0, waiting for transfers between devices: 69.1 us -> none  [the longest x1 24.3 us: local(): lax.all_to_all(sending[0], GRP_SUB, split_axis=0, concat_axis=0, tiled=True)]
    psum x5 -> x0, blocking collectives: 32.1 us -> none  [one_axis_at_a_time(): return functools.reduce(lax.psum, axes, x)]
    all_to_all x3 -> x0, starting transfers between devices: 22.9 us -> none  [the longest x1 11.9 us: local(): lax.all_to_all(sending[2], GRP_SUB, split_axis=0, concat_axis=0, tiled=True)]
    select_n x3 -> x0, local copies, waits for them, and re-layouts: 12.3 us -> none  [outbound(): return jnp.take(values.reshape(devices, block, width), inverse, axis=0)]
    gather x3 -> x0, local copies, waits for them, and re-layouts: 11.8 us -> none  [outbound(): return jnp.take(values.reshape(devices, block, width), inverse, axis=0)]
    reduce_sum x2 -> x1, other arithmetic: 7.95 us -> 0.76 us  [local(): jnp.sum(jnp.where(partner[None, :] == numbers[:, None], numbers[None, :],...]
    unnamed x4 -> x12, local copies, waits for them, and re-layouts: 0.58 us -> 7.49 us
  transfers between devices with their start and end apart: 3 -> 0, of which waited for: 3 -> 0; matrix products, arithmetic and copies ran while one was open for 6% -> 0% of each run, Pallas kernels for 0% -> 0%
where the time goes in v1:
time: 101 us; the launch traced here: 100 us
  Pallas kernels  91.3 us (90%)
  local copies, waits for them, and re-layouts  7.49 us (7%)
    pallas_call x1, Pallas kernels, local(): pl.pallas_call(exchange_kernel, out_shape=(block, block, block, block, pl...  88.8 us
    unnamed x12, local copies, waits for them, and re-layouts  7.49 us
    pallas_call x1, Pallas kernels, local(): pl.pallas_call(finish_kernel, out_shape=(whole,) * 3, in_specs=[vmem] * 5...  2.47 us

profile of v1, /device:TPU:1, one launch (start us, length us, event | category | flops | bytes accessed | tf_op | source)
XLA Modules:
  0.0 100.2 jit_solution(7943951957917044180)
XLA Ops:
  0.6 0.8 select_reduce_fusion.inverse
  1.4 0.0 copy-start
  1.4 1.5 %copy-done = f32[128,3584]{1,0:T(8,128)S(1)} copy-done((f32[128,3584]{1,0:T(8,128)S(1)}, f32[128,3584]{1,0:T(8,128)}, u32[]{:S(2)}) %copy-start) | copy-done | bytes 1835032
  2.9 0.0 copy-start.1
  2.9 1.5 %copy-done.1 = f32[128,3584]{1,0:T(8,128)S(1)} copy-done((f32[128,3584]{1,0:T(8,128)S(1)}, f32[128,3584]{1,0:T(8,128)}, u32[]{:S(2)}) %copy-start.1) | copy-done | bytes 1835032
  4.4 0.0 copy-start.2
  4.4 1.5 %copy-done.2 = f32[128,3584]{1,0:T(8,128)S(1)} copy-done((f32[128,3584]{1,0:T(8,128)S(1)}, f32[128,3584]{1,0:T(8,128)}, u32[]{:S(2)}) %copy-start.2) | copy-done | bytes 1835032
  5.9 0.0 copy-start.3
  5.9 1.5 %copy-done.3 = f32[128,3584]{1,0:T(8,128)S(1)} copy-done((f32[128,3584]{1,0:T(8,128)S(1)}, f32[128,3584]{1,0:T(8,128)}, u32[]{:S(2)}) %copy-start.3) | copy-done | bytes 1835032
  7.4 0.0 copy-start.4
  7.4 0.8 copy-done.4
  8.2 0.0 copy-start.5
  8.2 0.7 copy-done.5
  8.9 88.8 %exchange.1 = (f32[128,3584]{1,0:T(8,128)S(1)}, f32[128,3584]{1,0:T(8,128)S(1)}, f32[128,3584]{1,0:T(8,128)S(1)}, f32[128,3584]{1,0:T(8,128)S(1)}, f32[128,128]{1,0:T(8,128)S(1)}) custom-call(s32[128]{0:T(128)S(1)} %select_reduce_fusion.inverse, s32[1,128]{1,0:T(1,128)S(1)} %bitcast.3, s32[128,128]{1,0:T(8,128)S(1)} %bitcast.2, f32[128,3584]{1,0:T(8,128)S(1)} %copy-done, ...), custom_call_target="tpu_custom_call" | custom-call | tf_op jit(solution)/shard_map/exchange/pallas_call | solution.py:229
  97.8 2.5 %finish.1 = (f32[128,3584]{1,0:T(8,128)}, f32[128,3584]{1,0:T(8,128)}, f32[128,3584]{1,0:T(8,128)}) custom-call(f32[128,3584]{1,0:T(8,128)S(1)} %get-tuple-element.8.weights, f32[128,3584]{1,0:T(8,128)S(1)} %get-tuple-element.9.update, f32[128,3584]{1,0:T(8,128)S(1)} %get-tuple-element.10.first, f32[128,3584]{1,0:T(8,128)S(1)} %get-tuple-element.11.second, ...), custom_call_target="tpu_custom_call" | custom-call | tf_op jit(solution)/shard_map/finish/pallas_call | solution.py:254
Async XLA Ops:
  1.4 1.5 %copy-start = (f32[128,3584]{1,0:T(8,128)S(1)}, f32[128,3584]{1,0:T(8,128)}, u32[]{:S(2)}) copy-start(f32[128,3584]{1,0:T(8,128)} %master.1) | copy-start | bytes 5505028
  2.9 1.5 %copy-start.1 = (f32[128,3584]{1,0:T(8,128)S(1)}, f32[128,3584]{1,0:T(8,128)}, u32[]{:S(2)}) copy-start(f32[128,3584]{1,0:T(8,128)} %moment_one.1) | copy-start | bytes 5505028
  4.4 1.5 %copy-start.2 = (f32[128,3584]{1,0:T(8,128)S(1)}, f32[128,3584]{1,0:T(8,128)}, u32[]{:S(2)}) copy-start(f32[128,3584]{1,0:T(8,128)} %moment_two.1) | copy-start | bytes 5505028
  5.9 1.5 %copy-start.3 = (f32[128,3584]{1,0:T(8,128)S(1)}, f32[128,3584]{1,0:T(8,128)}, u32[]{:S(2)}) copy-start(f32[128,3584]{1,0:T(8,128)} %gradient.1) | copy-start | bytes 5505028
  7.4 0.8 copy-start.4
  8.2 0.7 copy-start.5

commit v2 on v1

--- a/solution.py
+++ b/solution.py
@@ -38,10 +38,10 @@
 
 
 def exchange_kernel(
-    inverse, partner, row_tensor, master, moment_one, moment_two, gradient,
+    partner, tensor_of_row, master, moment_one, moment_two, gradient,
     weights, update, first, second, row_ratio,
-    source, sending, spare, ids, partial, totals,
-    load_sem, grad_sem, send_sem, recv_sem, total_send_sem, total_recv_sem,
+    source, sending, spare, row_tensor, ids, partner_row, inverse_row, inverse, partial, totals,
+    load_sem, partner_sem, tensor_sem, grad_sem, send_sem, recv_sem, total_send_sem, total_recv_sem,
 ):
     devices, width = weights.shape
     blocks = devices // GROUP
@@ -55,6 +55,8 @@
             (x + offset // 32) % 4, (y + offset // 8 % 4) % 4, (z + offset // 2 % 4) % 4, (core + offset % 2) % 2
         )
 
+    partner_load = pltpu.make_async_copy(partner, partner_row, partner_sem)
+    partner_load.start()
     loads = [
         pltpu.make_async_copy(array, source.at[k], load_sem.at[k])
         for k, array in enumerate((master, moment_one, moment_two))
@@ -63,6 +65,8 @@
         load.start()
     grad_load = pltpu.make_async_copy(gradient, update, grad_sem)
     grad_load.start()
+    tensor_load = pltpu.make_async_copy(tensor_of_row, row_tensor, tensor_sem)
+    tensor_load.start()
 
     barrier = pltpu.get_barrier_semaphore()
 
@@ -72,15 +76,25 @@
 
     lax.fori_loop(1, devices, greet, 0)
 
-    held = lax.broadcasted_iota(jnp.int32, (devices, devices), 1)
-    mine = jnp.where(partner[...] == me, row_tensor[...] + held * 0, 0)
+    down = lax.broadcasted_iota(jnp.int32, (devices, devices), 0)
+    across = lax.broadcasted_iota(jnp.int32, (devices, devices), 1)
+    partner_load.wait()
+    places = jnp.broadcast_to(partner_row[...], (devices, devices))
+    rank_of = jnp.sum(jnp.where(places == down, across, 0), axis=1, keepdims=True)
+    turned = jnp.sum(jnp.where(down == across, rank_of, 0), axis=0, keepdims=True)
+    inverse_row[...] = jnp.broadcast_to(turned, (GROUP, devices))
+    inverse_move = pltpu.make_async_copy(inverse_row.at[pl.ds(0, 1)], inverse, partner_sem)
+    inverse_move.start()
+    tensor_load.wait()
+    mine = jnp.where(places == me, row_tensor[...], 0)
     ids[...] = jnp.broadcast_to(jnp.sum(mine, axis=1, keepdims=True), (devices, LANES))
+    inverse_move.wait()
 
     for load in loads:
         load.wait()
 
     def pick(step):
-        row = inverse[target(step)]
+        row = inverse[0, target(step)] & (devices - 1)
         for k in range(3):
             sending[k, pl.ds(step, 1), :] = source[k, pl.ds(row, 1), :]
 
@@ -218,27 +232,34 @@
 def local(master, moment_one, moment_two, gradient, partner, tensor_of_row):
     rows_dev, width = master.shape
     devices = partner.shape[0]
-    numbers = jnp.arange(devices, dtype=jnp.int32)
-    inverse = jnp.sum(jnp.where(partner[None, :] == numbers[:, None], numbers[None, :], 0), axis=1)
+    operands = (
+        partner.reshape(1, devices), tensor_of_row.reshape(devices, devices), master, moment_one, moment_two, gradient
+    )
+    operands = [pltpu.with_memory_space_constraint(operand, pltpu.HBM) for operand in operands]
     vmem = pl.BlockSpec(memory_space=pltpu.VMEM)
     hbm = pl.BlockSpec(memory_space=pltpu.HBM)
-    smem = pl.BlockSpec(memory_space=pltpu.SMEM)
     block = pltpu.VMEM((rows_dev, width), jnp.float32)
     stack = pltpu.VMEM((3, rows_dev, width), jnp.float32)
     dma = pltpu.SemaphoreType.DMA
     weights, update, first, second, row_ratio = pl.pallas_call(
         exchange_kernel,
         out_shape=(block, block, block, block, pltpu.VMEM((rows_dev, LANES), jnp.float32)),
-        in_specs=[smem, vmem, vmem, hbm, hbm, hbm, hbm],
+        in_specs=[hbm] * 6,
         out_specs=(vmem,) * 5,
         scratch_shapes=[
             stack,
             stack,
             pltpu.VMEM((3, GROUP, width), jnp.float32),
+            pltpu.VMEM((devices, devices), jnp.int32),
             pltpu.VMEM((rows_dev, LANES), jnp.int32),
+            pltpu.VMEM((1, devices), jnp.int32),
+            pltpu.VMEM((GROUP, devices), jnp.int32),
+            pltpu.SMEM((1, devices), jnp.int32),
             pltpu.VMEM((GROUP, LANES), jnp.float32),
             pltpu.VMEM((devices, LANES), jnp.float32),
             dma((3,)),
+            dma,
+            dma,
             dma,
             dma,
             dma((devices // GROUP,)),
@@ -249,7 +270,7 @@
             collective_id=0, has_side_effects=True, vmem_limit_bytes=24 * 1024 * 1024
         ),
         name="exchange",
-    )(inverse, partner.reshape(1, devices), tensor_of_row.reshape(devices, devices), master, moment_one, moment_two, gradient)
+    )(*operands)
     whole = jax.ShapeDtypeStruct((rows_dev, width), jnp.float32)
     return pl.pallas_call(
         finish_kernel,

time: 101 us -> 91.1 us (0.902)
  local copies, waits for them, and re-layouts: 7.49 us -> 0 us
    unnamed x12 -> x0, local copies, waits for them, and re-layouts: 7.49 us -> none
where the time goes in v2:
time: 91.1 us; the launch traced here: 91 us
  Pallas kernels  90.4 us (99%)
    pallas_call x1, Pallas kernels, local(): pl.pallas_call(exchange_kernel, out_shape=(block, block, block, block, pl...  87.9 us
    pallas_call x1, Pallas kernels, local(): pl.pallas_call(finish_kernel, out_shape=(whole,) * 3, in_specs=[vmem] * 5...  2.47 us

profile of v2, /device:TPU:1, one launch (start us, length us, event | category | flops | bytes accessed | tf_op | source)
XLA Modules:
  0.0 91.0 jit_solution(1697474038223454424)
XLA Ops:
  0.6 87.9 %exchange.1 = (f32[128,3584]{1,0:T(8,128)S(1)}, f32[128,3584]{1,0:T(8,128)S(1)}, f32[128,3584]{1,0:T(8,128)S(1)}, f32[128,3584]{1,0:T(8,128)S(1)}, f32[128,128]{1,0:T(8,128)S(1)}) custom-call(s32[1,128]{1,0:T(1,128)} %bitcast.3, s32[128,128]{1,0:T(8,128)} %bitcast.2, f32[128,3584]{1,0:T(8,128)} %master.1, f32[128,3584]{1,0:T(8,128)} %moment_one.1, ...), custom_call_target="tpu_custom_call" | custom-call | tf_op jit(solution)/shard_map/exchange/pallas_call | solution.py:244
  88.6 2.5 %finish.1 = (f32[128,3584]{1,0:T(8,128)}, f32[128,3584]{1,0:T(8,128)}, f32[128,3584]{1,0:T(8,128)}) custom-call(f32[128,3584]{1,0:T(8,128)S(1)} %get-tuple-element.8.weights, f32[128,3584]{1,0:T(8,128)S(1)} %get-tuple-element.9.update, f32[128,3584]{1,0:T(8,128)S(1)} %get-tuple-element.10.first, f32[128,3584]{1,0:T(8,128)S(1)} %get-tuple-element.11.second, ...), custom_call_target="tpu_custom_call" | custom-call | tf_op jit(solution)/shard_map/finish/pallas_call | solution.py:275

commit v3 on v2

--- a/solution.py
+++ b/solution.py
@@ -49,11 +49,25 @@
     me = number_of(x, y, z, core)
     arrived = (weights, first, second)
 
+    turn = 1 - 2 * core
+
     def target(step):
         offset = (step * STRIDE) % devices
         return number_of(
-            (x + offset // 32) % 4, (y + offset // 8 % 4) % 4, (z + offset // 2 % 4) % 4, (core + offset % 2) % 2
+            (x + turn * (offset // 32) + 4) % 4,
+            (y + turn * (offset // 8 % 4) + 4) % 4,
+            (z + turn * (offset // 2 % 4) + 4) % 4,
+            (core + offset % 2) % 2,
         )
+
+    x_part = [((x + d) % 4) * 4 for d in range(4)]
+    y_part = [((y + d) % 4) * 32 for d in range(4)]
+    z_part = [((z + d) % 4) // 2 * 16 + ((z + d) % 4) % 2 * 2 for d in range(4)]
+    core_part = [(core + d) % 2 for d in range(2)]
+    places = [(dx, dy, dz, dc) for dx in range(4) for dy in range(4) for dz in range(4) for dc in range(2)]
+    places.remove((0, 0, 0, 0))
+    places.sort(key=lambda d: sum(min(v, 4 - v) for v in d[:3]), reverse=True)
+    others = [x_part[dx] + y_part[dy] + z_part[dz] + core_part[dc] for dx, dy, dz, dc in places]
 
     partner_load = pltpu.make_async_copy(partner, partner_row, partner_sem)
     partner_load.start()
@@ -70,23 +84,20 @@
 
     barrier = pltpu.get_barrier_semaphore()
 
-    def greet(step, carry):
-        pl.semaphore_signal(barrier, inc=1, device_id=(me + step) % devices, device_id_type=LOGICAL)
-        return carry
-
-    lax.fori_loop(1, devices, greet, 0)
+    for other in others:
+        pl.semaphore_signal(barrier, inc=1, device_id=other, device_id_type=LOGICAL)
 
     down = lax.broadcasted_iota(jnp.int32, (devices, devices), 0)
     across = lax.broadcasted_iota(jnp.int32, (devices, devices), 1)
     partner_load.wait()
-    places = jnp.broadcast_to(partner_row[...], (devices, devices))
-    rank_of = jnp.sum(jnp.where(places == down, across, 0), axis=1, keepdims=True)
+    holder = jnp.broadcast_to(partner_row[...], (devices, devices))
+    rank_of = jnp.sum(jnp.where(holder == down, across, 0), axis=1, keepdims=True)
     turned = jnp.sum(jnp.where(down == across, rank_of, 0), axis=0, keepdims=True)
     inverse_row[...] = jnp.broadcast_to(turned, (GROUP, devices))
     inverse_move = pltpu.make_async_copy(inverse_row.at[pl.ds(0, 1)], inverse, partner_sem)
     inverse_move.start()
     tensor_load.wait()
-    mine = jnp.where(places == me, row_tensor[...], 0)
+    mine = jnp.where(holder == me, row_tensor[...], 0)
     ids[...] = jnp.broadcast_to(jnp.sum(mine, axis=1, keepdims=True), (devices, LANES))
     inverse_move.wait()
 
@@ -110,9 +121,6 @@
                 device_id_type=LOGICAL,
             ).start()
 
-    for step in range(GROUP):
-        pick(step)
-    pl.semaphore_wait(barrier, devices - 1)
 
     def keep():
         for k in range(3):
@@ -125,7 +133,9 @@
         for j in range(GROUP):
             pick(group * GROUP + j)
 
+    pick_group(0)
     pick_group(1)
+    pl.semaphore_wait(barrier, devices - 1)
     keep()
     for step in range(1, GROUP):
         send(step)
@@ -182,18 +192,15 @@
             packed = jnp.where(lane_id == t + LAYERS * part, jnp.sum(sums[t][part]), packed)
     partial[...] = jnp.broadcast_to(packed, (GROUP, LANES))
 
-    def tell(step, carry):
+    for other in others:
         pltpu.make_async_remote_copy(
             src_ref=partial.at[pl.ds(0, 1)],
             dst_ref=totals.at[pl.ds(me, 1)],
             send_sem=total_send_sem,
             recv_sem=total_recv_sem,
-            device_id=target(step),
+            device_id=other,
             device_id_type=LOGICAL,
         ).start()
-        return carry
-
-    lax.fori_loop(1, devices, tell, 0)
     pltpu.make_async_copy(partial.at[pl.ds(0, 1)], totals.at[pl.ds(me, 1)], total_recv_sem).start()
     pltpu.make_async_copy(partial.at[pl.ds(0, 1)], spare.at[0, pl.ds(1, 1), pl.ds(0, LANES)], total_send_sem).start()
     pltpu.make_async_copy(totals, totals, total_recv_sem).wait()
@@ -209,12 +216,14 @@
 
 def finish_kernel(weights, update, first, second, row_ratio, new_master, new_one, new_two, fresh, sem_one, sem_two, sem_fresh):
     rows, width = weights.shape
-    one = pltpu.make_async_copy(first, new_one, sem_one)
-    two = pltpu.make_async_copy(second, new_two, sem_two)
-    one.start()
-    two.start()
     chunk = 32
     writes = []
+    for index in range(rows // chunk):
+        at = pl.ds(index * chunk, chunk)
+        writes.append(pltpu.make_async_copy(first.at[at], new_one.at[at], sem_one.at[index]))
+        writes.append(pltpu.make_async_copy(second.at[at], new_two.at[at], sem_two.at[index]))
+    for write in writes:
+        write.start()
     for index in range(rows // chunk):
         at = pl.ds(index * chunk, chunk)
         scale = learn_rate * row_ratio[at, :]
@@ -225,8 +234,6 @@
         writes[-1].start()
     for write in writes:
         write.wait()
-    one.wait()
-    two.wait()
 
 
 def local(master, moment_one, moment_two, gradient, partner, tensor_of_row):
@@ -277,7 +284,7 @@
         out_shape=(whole,) * 3,
         in_specs=[vmem] * 5,
         out_specs=(hbm,) * 3,
-        scratch_shapes=[block, dma, dma, dma((4,))],
+        scratch_shapes=[block, dma((4,)), dma((4,)), dma((4,))],
         compiler_params=pltpu.CompilerParams(vmem_limit_bytes=8 * 1024 * 1024),
         name="finish",
     )(weights, update, first, second, row_ratio)

time: 91.1 us -> 84.3 us (0.925)
  Pallas kernels: 90.4 us -> 83.6 us
    pallas_call x1, Pallas kernels: 87.9 us -> 81.1 us  [local(): pl.pallas_call(exchange_kernel, out_shape=(block, block, block, block, pl...]
where the time goes in v3:
time: 84.3 us; the launch traced here: 84.2 us
  Pallas kernels  83.6 us (99%)
    pallas_call x1, Pallas kernels, local(): pl.pallas_call(exchange_kernel, out_shape=(block, block, block, block, pl...  81.1 us
    pallas_call x1, Pallas kernels, local(): pl.pallas_call(finish_kernel, out_shape=(whole,) * 3, in_specs=[vmem] * 5...  2.52 us

profile of v3, /device:TPU:1, one launch (start us, length us, event | category | flops | bytes accessed | tf_op | source)
XLA Modules:
  0.0 84.2 jit_solution(6579017817130315330)
XLA Ops:
  0.6 81.1 %exchange.1 = (f32[128,3584]{1,0:T(8,128)S(1)}, f32[128,3584]{1,0:T(8,128)S(1)}, f32[128,3584]{1,0:T(8,128)S(1)}, f32[128,3584]{1,0:T(8,128)S(1)}, f32[128,128]{1,0:T(8,128)S(1)}) custom-call(s32[1,128]{1,0:T(1,128)} %bitcast.3, s32[128,128]{1,0:T(8,128)} %bitcast.2, f32[128,3584]{1,0:T(8,128)} %master.1, f32[128,3584]{1,0:T(8,128)} %moment_one.1, ...), custom_call_target="tpu_custom_call" | custom-call | tf_op jit(solution)/shard_map/exchange/pallas_call | solution.py:251
  81.7 2.5 %finish.1 = (f32[128,3584]{1,0:T(8,128)}, f32[128,3584]{1,0:T(8,128)}, f32[128,3584]{1,0:T(8,128)}) custom-call(f32[128,3584]{1,0:T(8,128)S(1)} %get-tuple-element.8.weights, f32[128,3584]{1,0:T(8,128)S(1)} %get-tuple-element.9.update, f32[128,3584]{1,0:T(8,128)S(1)} %get-tuple-element.10.first, f32[128,3584]{1,0:T(8,128)S(1)} %get-tuple-element.11.second, ...), custom_call_target="tpu_custom_call" | custom-call | tf_op jit(solution)/shard_map/finish/pallas_call | solution.py:282

commit v4 on v3

--- a/solution.py
+++ b/solution.py
@@ -14,6 +14,10 @@
 STRIDE = 37
 LANES = 128
 GROUP = 8
+BLOCK_ORDER = (
+    (2, 0, 0), (2, 0, 1), (2, 1, 0), (2, 1, 1), (1, 1, 1), (3, 1, 1), (1, 0, 1), (1, 1, 0),
+    (3, 0, 1), (3, 1, 0), (0, 1, 1), (1, 0, 0), (3, 0, 0), (0, 0, 1), (0, 1, 0), (0, 0, 0),
+)
 
 
 beta_one = 0.9
@@ -50,6 +54,10 @@
     arrived = (weights, first, second)
 
     turn = 1 - 2 * core
+
+    def spread(step):
+        offset = (step * STRIDE) % devices
+        return sum(d * (4 - d) for d in (offset // 32, offset // 8 % 4, offset // 2 % 4))
 
     def target(step):
         offset = (step * STRIDE) % devices
@@ -138,23 +146,35 @@
     pl.semaphore_wait(barrier, devices - 1)
     keep()
     for step in range(1, GROUP):
-        send(step)
+        if spread(step) > 3:
+            send(step)
+
+    def send_far(step):
+        @pl.when(spread(step) > 3)
+        def _():
+            send(step)
 
     def round_of(group, carry):
         pick_group(group + 1)
         for j in range(GROUP):
-            send(group * GROUP + j)
+            send_far(group * GROUP + j)
         return carry
 
     lax.fori_loop(1, blocks - 1, round_of, 0)
-    for j in range(GROUP):
-        send((blocks - 1) * GROUP + j)
+    for step in range((blocks - 1) * GROUP, devices):
+        if spread(step) > 3:
+            send(step)
+    for step in range(1, devices):
+        if spread(step) <= 3:
+            send(step)
 
     grad_load.wait()
     scale_one = 1.0 / (1.0 - beta_one**step_count)
     scale_two = 1.0 / (1.0 - beta_two**step_count)
 
-    def compute(block, sums):
+    def compute(_, carry):
+        y_code, z_code, x_code, sums = carry
+        block = ((y + y_code % 4) % 4 * 2 + (z // 2 + z_code % 2) % 2) * 2 + (x // 2 + x_code % 2) % 2
         pltpu.make_async_copy(
             sending.at[0, pl.ds(0, 3 * GROUP)], source.at[0, pl.ds(0, 3 * GROUP)], recv_sem.at[block]
         ).wait()
@@ -174,16 +194,19 @@
             row_update += step * step
             row_weight += weight * weight
         tensor = ids[rows, :]
-        return tuple(
+        sums = tuple(
             (
                 sums[t][0] + jnp.where(tensor == t, row_update, 0.0),
                 sums[t][1] + jnp.where(tensor == t, row_weight, 0.0),
             )
             for t in range(LAYERS)
         )
+        return y_code // 4, z_code // 2, x_code // 2, sums
 
     zero = jnp.zeros((GROUP, LANES), jnp.float32)
-    sums = lax.fori_loop(0, blocks, compute, tuple((zero, zero) for _ in range(LAYERS)))
+    codes = [sum(d[i] * base**k for k, d in enumerate(BLOCK_ORDER)) for i, base in enumerate((4, 2, 2))]
+    carry = (*[jnp.int32(code) for code in codes], tuple((zero, zero) for _ in range(LAYERS)))
+    sums = lax.fori_loop(0, blocks, compute, carry)[3]
 
     lane_id = lax.broadcasted_iota(jnp.int32, (1, LANES), 1)
     packed = jnp.zeros((1, LANES), jnp.float32)

time: 84.3 us -> 83.1 us (0.986)
  Pallas kernels: 83.6 us -> 82.4 us
    pallas_call x1, Pallas kernels: 81.1 us -> 79.9 us  [local(): pl.pallas_call(exchange_kernel, out_shape=(block, block, block, block, pl...]
where the time goes in v4:
time: 83.1 us; the launch traced here: 83 us
  Pallas kernels  82.4 us (99%)
    pallas_call x1, Pallas kernels, local(): pl.pallas_call(exchange_kernel, out_shape=(block, block, block, block, pl...  79.9 us
    pallas_call x1, Pallas kernels, local(): pl.pallas_call(finish_kernel, out_shape=(whole,) * 3, in_specs=[vmem] * 5...  2.52 us

profile of v4, /device:TPU:1, one launch (start us, length us, event | category | flops | bytes accessed | tf_op | source)
XLA Modules:
  0.0 83.0 jit_solution(7821074078411934784)
XLA Ops:
  0.6 79.9 %exchange.1 = (f32[128,3584]{1,0:T(8,128)S(1)}, f32[128,3584]{1,0:T(8,128)S(1)}, f32[128,3584]{1,0:T(8,128)S(1)}, f32[128,3584]{1,0:T(8,128)S(1)}, f32[128,128]{1,0:T(8,128)S(1)}) custom-call(s32[1,128]{1,0:T(1,128)} %bitcast.3, s32[128,128]{1,0:T(8,128)} %bitcast.2, f32[128,3584]{1,0:T(8,128)} %master.1, f32[128,3584]{1,0:T(8,128)} %moment_one.1, ...), custom_call_target="tpu_custom_call" | custom-call | tf_op jit(solution)/shard_map/exchange/pallas_call | solution.py:274
  80.5 2.5 %finish.1 = (f32[128,3584]{1,0:T(8,128)}, f32[128,3584]{1,0:T(8,128)}, f32[128,3584]{1,0:T(8,128)}) custom-call(f32[128,3584]{1,0:T(8,128)S(1)} %get-tuple-element.8.weights, f32[128,3584]{1,0:T(8,128)S(1)} %get-tuple-element.9.update, f32[128,3584]{1,0:T(8,128)S(1)} %get-tuple-element.10.first, f32[128,3584]{1,0:T(8,128)S(1)} %get-tuple-element.11.second, ...), custom_call_target="tpu_custom_call" | custom-call | tf_op jit(solution)/shard_map/finish/pallas_call | solution.py:305

commit v5 on v4

--- a/solution.py
+++ b/solution.py
@@ -11,7 +11,7 @@
 LAYERS = 8
 AXES = ("grp_0", "grp_1", "grp_2", "sub_0", "sub_1")
 LOGICAL = pl.DeviceIdType.LOGICAL
-STRIDE = 37
+STRIDE = 19
 LANES = 128
 GROUP = 8
 BLOCK_ORDER = (
@@ -57,15 +57,15 @@
 
     def spread(step):
         offset = (step * STRIDE) % devices
-        return sum(d * (4 - d) for d in (offset // 32, offset // 8 % 4, offset // 2 % 4))
+        return sum(d * (4 - d) for d in (offset // 16 % 4, offset // 4 % 4, offset // 1 % 4))
 
     def target(step):
         offset = (step * STRIDE) % devices
         return number_of(
-            (x + turn * (offset // 32) + 4) % 4,
-            (y + turn * (offset // 8 % 4) + 4) % 4,
-            (z + turn * (offset // 2 % 4) + 4) % 4,
-            (core + offset % 2) % 2,
+            (x + turn * (offset // 16 % 4) + 4) % 4,
+            (y + turn * (offset // 4 % 4) + 4) % 4,
+            (z + turn * (offset // 1 % 4) + 4) % 4,
+            (core + offset // 64 % 2) % 2,
         )
 
     x_part = [((x + d) % 4) * 4 for d in range(4)]
@@ -208,11 +208,16 @@
     carry = (*[jnp.int32(code) for code in codes], tuple((zero, zero) for _ in range(LAYERS)))
     sums = lax.fori_loop(0, blocks, compute, carry)[3]
 
-    lane_id = lax.broadcasted_iota(jnp.int32, (1, LANES), 1)
-    packed = jnp.zeros((1, LANES), jnp.float32)
+    kinds = 2 * LAYERS
+    kind_id = lax.broadcasted_iota(jnp.int32, (kinds, LANES), 0)
+    lane_id = lax.broadcasted_iota(jnp.int32, (kinds, LANES), 1)
+    stacked = jnp.zeros((kinds, LANES), jnp.float32)
     for t in range(LAYERS):
         for part in range(2):
-            packed = jnp.where(lane_id == t + LAYERS * part, jnp.sum(sums[t][part]), packed)
+            folded = jnp.sum(sums[t][part], axis=0, keepdims=True)
+            stacked = jnp.where(kind_id == t + LAYERS * part, folded, stacked)
+    column = jnp.sum(stacked, axis=1, keepdims=True)
+    packed = jnp.sum(jnp.where(kind_id == lane_id, column, 0.0), axis=0, keepdims=True)
     partial[...] = jnp.broadcast_to(packed, (GROUP, LANES))
 
     for other in others:

time: 83.1 us -> 82.5 us (level)
  no operation moved by 1% of the time
where the time goes in v5:
time: 82.5 us; the launch traced here: 82.4 us
  Pallas kernels  81.8 us (99%)
    pallas_call x1, Pallas kernels, local(): pl.pallas_call(exchange_kernel, out_shape=(block, block, block, block, pl...  79.3 us
    pallas_call x1, Pallas kernels, local(): pl.pallas_call(finish_kernel, out_shape=(whole,) * 3, in_specs=[vmem] * 5...  2.52 us

profile of v5, /device:TPU:1, one launch (start us, length us, event | category | flops | bytes accessed | tf_op | source)
XLA Modules:
  0.0 82.4 jit_solution(5946966375040567804)
XLA Ops:
  0.6 79.3 %exchange.1 = (f32[128,3584]{1,0:T(8,128)S(1)}, f32[128,3584]{1,0:T(8,128)S(1)}, f32[128,3584]{1,0:T(8,128)S(1)}, f32[128,3584]{1,0:T(8,128)S(1)}, f32[128,128]{1,0:T(8,128)S(1)}) custom-call(s32[1,128]{1,0:T(1,128)} %bitcast.3, s32[128,128]{1,0:T(8,128)} %bitcast.2, f32[128,3584]{1,0:T(8,128)} %master.1, f32[128,3584]{1,0:T(8,128)} %moment_one.1, ...), custom_call_target="tpu_custom_call" | custom-call | tf_op jit(solution)/shard_map/exchange/pallas_call | solution.py:279
  79.9 2.5 %finish.1 = (f32[128,3584]{1,0:T(8,128)}, f32[128,3584]{1,0:T(8,128)}, f32[128,3584]{1,0:T(8,128)}) custom-call(f32[128,3584]{1,0:T(8,128)S(1)} %get-tuple-element.8.weights, f32[128,3584]{1,0:T(8,128)S(1)} %get-tuple-element.9.update, f32[128,3584]{1,0:T(8,128)S(1)} %get-tuple-element.10.first, f32[128,3584]{1,0:T(8,128)S(1)} %get-tuple-element.11.second, ...), custom_call_target="tpu_custom_call" | custom-call | tf_op jit(solution)/shard_map/finish/pallas_call | solution.py:310

commit v6 on v5

--- a/solution.py
+++ b/solution.py
@@ -15,8 +15,8 @@
 LANES = 128
 GROUP = 8
 BLOCK_ORDER = (
-    (2, 0, 0), (2, 0, 1), (2, 1, 0), (2, 1, 1), (1, 1, 1), (3, 1, 1), (1, 0, 1), (1, 1, 0),
-    (3, 0, 1), (3, 1, 0), (0, 1, 1), (1, 0, 0), (3, 0, 0), (0, 0, 1), (0, 1, 0), (0, 0, 0),
+    (2, 0, 0), (0, 1, 1), (1, 1, 0), (3, 1, 0), (1, 1, 1), (3, 1, 1), (2, 1, 0), (1, 0, 1),
+    (3, 0, 1), (2, 0, 1), (2, 1, 1), (0, 1, 0), (1, 0, 0), (3, 0, 0), (0, 0, 1), (0, 0, 0),
 )
 
 

time: 82.5 us -> 83.1 us (level)
  no operation moved by 1% of the time
where the time goes in v6:
time: 83.1 us; the launch traced here: 83 us
  Pallas kernels  82.4 us (99%)
    pallas_call x1, Pallas kernels, local(): pl.pallas_call(exchange_kernel, out_shape=(block, block, block, block, pl...  79.9 us
    pallas_call x1, Pallas kernels, local(): pl.pallas_call(finish_kernel, out_shape=(whole,) * 3, in_specs=[vmem] * 5...  2.52 us

profile of v6, /device:TPU:1, one launch (start us, length us, event | category | flops | bytes accessed | tf_op | source)
XLA Modules:
  0.0 83.0 jit_solution(3272009156627357731)
XLA Ops:
  0.6 79.9 %exchange.1 = (f32[128,3584]{1,0:T(8,128)S(1)}, f32[128,3584]{1,0:T(8,128)S(1)}, f32[128,3584]{1,0:T(8,128)S(1)}, f32[128,3584]{1,0:T(8,128)S(1)}, f32[128,128]{1,0:T(8,128)S(1)}) custom-call(s32[1,128]{1,0:T(1,128)} %bitcast.3, s32[128,128]{1,0:T(8,128)} %bitcast.2, f32[128,3584]{1,0:T(8,128)} %master.1, f32[128,3584]{1,0:T(8,128)} %moment_one.1, ...), custom_call_target="tpu_custom_call" | custom-call | tf_op jit(solution)/shard_map/exchange/pallas_call | solution.py:279
  80.5 2.5 %finish.1 = (f32[128,3584]{1,0:T(8,128)}, f32[128,3584]{1,0:T(8,128)}, f32[128,3584]{1,0:T(8,128)}) custom-call(f32[128,3584]{1,0:T(8,128)S(1)} %get-tuple-element.8.weights, f32[128,3584]{1,0:T(8,128)S(1)} %get-tuple-element.9.update, f32[128,3584]{1,0:T(8,128)S(1)} %get-tuple-element.10.first, f32[128,3584]{1,0:T(8,128)S(1)} %get-tuple-element.11.second, ...), custom_call_target="tpu_custom_call" | custom-call | tf_op jit(solution)/shard_map/finish/pallas_call | solution.py:310
